TPU v7x, 32 devices: a whole 2x2x4 slice. The times are simulated.
32 devices in a mesh: dom: 8 (over z, y), slab: 4 (over x, core).
Axes of the slice: x: 2, y: 2, z: 4, core: 2. Of those that a mesh axis runs over, the one named last changes fastest.
Arguments:
- particles: bfloat16 [1536, 32, 1024], P('dom', 'slab'), may hold values from -6 to 6
- refs: bfloat16 [2048, 32, 2048], P('dom', 'slab'), may hold values from -6 to 6
- orient: int32 [1536], P('dom'), may hold values from 0 to 2047, as said below
- shifts: int32 [1536, 8, 2], P('dom'), may hold values from -4 to 4
- tilt: int32 [1536], P('dom'), may hold values from 0 to 15
- wedge: float32 [16, 32, 1024], P(None, 'slab'), may hold values from 0.1 to 1
Outputs:
- new_refs: float32 [2048, 32, 2048], P('dom', 'slab')
- shift_weights: float32 [1536, 8], P('dom')
Inputs may be any that keep to these rules, and one draw needn't show every extreme that they name: `orient`: split the particles into aligned blocks of 192 (the rows of one device) and the orientations into ranges of 256. In every block at most 48 particles have orientations in any one range, and in every draw one range holds exactly 48 particles of every block.
All inputs are finite; a program needn't handle non-finite values.
Results may differ from a plain program's by a relative error of at most 0.004.
Values may be sent and summed in bfloat16 or wider, within the bound.
A program may use at most 128 MiB of HBM per device.

v0:
```python
import functools
import math

import jax
import jax.numpy as jnp
from jax import lax
from jax.experimental import pallas as pl
from jax.experimental.pallas import tpu as pltpu
from jax.sharding import PartitionSpec as P

BOX = 32
CHUNKS = 6
BINS = 128

MESH = pl.DeviceIdType.MESH
HIGH = lax.Precision.HIGHEST
VMEM_SPEC = pl.BlockSpec(memory_space=pltpu.VMEM)
SMEM_SPEC = pl.BlockSpec(memory_space=pltpu.SMEM)
ANY_SPEC = pl.BlockSpec(memory_space=pl.ANY)


def phase_rows(rows, cols, row_at, col_at, box):
    pixel = lax.broadcasted_iota(jnp.int32, (rows, cols), 0) + row_at
    freq = lax.broadcasted_iota(jnp.int32, (rows, cols), 1) + col_at
    phase = ((pixel // box) * (freq // box) + (pixel % box) * (freq % box)) % box
    return phase.astype(jnp.float32) * (2.0 * math.pi / box)


def shift_rows(cols, box):
    bins = lax.broadcasted_iota(jnp.int32, (BINS, cols), 0)
    freq = lax.broadcasted_iota(jnp.int32, (BINS, cols), 1)
    phase = ((bins // 9 - 4) * (freq // box) + (bins % 9 - 4) * (freq % box) + 32 * box) % box
    return phase.astype(jnp.float32) * (2.0 * math.pi / box)


def exchange_kernel(
    peers, holder_ref, from_ref, meta_ref, refs_ref,
    spec_ref, every_ref, in_meta_ref, steer_ref,
    out_ref, rows, table, got, q, stage, index_ref,
    send, recv, own_sem, meta_send, meta_recv, local_sem, spec_sem,
):
    chunks, _, each, planes, volume = out_ref.shape
    n = peers * each
    me = lax.axis_index("dom")
    barrier = pltpu.get_barrier_semaphore()
    for k in range(1, peers):
        pl.semaphore_signal(
            barrier, inc=1, device_id={"dom": lax.rem(me + k, peers)}, device_id_type=MESH
        )
    pl.semaphore_wait(barrier, peers - 1)

    def meta_copy(k):
        to = lax.rem(me + k, peers)
        return pltpu.make_async_remote_copy(
            src_ref=meta_ref.at[to], dst_ref=in_meta_ref.at[me],
            send_sem=meta_send.at[k], recv_sem=meta_recv.at[k],
            device_id={"dom": to}, device_id_type=MESH,
        )

    def row_copy(c, k):
        to = lax.rem(me + k, peers)
        return pltpu.make_async_remote_copy(
            src_ref=out_ref.at[c, to], dst_ref=rows.at[c, me],
            send_sem=send.at[c, k], recv_sem=recv.at[c, k],
            device_id={"dom": to}, device_id_type=MESH,
        )

    def start_meta(k, carry):
        meta_copy(k).start()
        return carry

    lax.fori_loop(1, peers, start_meta, 0)

    def pick_chunk(c, carry):
        def pick_owner(k, carry):
            to = lax.rem(me + k, peers)
            for j in range(each):
                out_ref[c, to, j] = from_ref[holder_ref[c * n + to * each + j]]
            return carry

        def start_rows(k, carry):
            row_copy(c, k).start()
            return carry

        lax.fori_loop(0, peers, pick_owner, 0)
        lax.fori_loop(1, peers, start_rows, 0)
        return carry

    lax.fori_loop(0, chunks, pick_chunk, 0)
    own_meta = pltpu.make_async_copy(meta_ref.at[me], in_meta_ref.at[me], local_sem)
    own_meta.start()
    own = pltpu.make_async_copy(out_ref.at[:, me], rows.at[:, me], own_sem)
    own.start()

    tile = 128

    def fill(i, carry):
        at = pl.multiple_of(i * tile, tile)
        for j in range(0, volume, tile):
            angle = phase_rows(tile, tile, at, j, BOX)
            table[pl.ds(at, tile), j : j + tile] = jnp.cos(angle).astype(jnp.bfloat16)
            table[pl.ds(at, tile), volume + j : volume + j + tile] = (-jnp.sin(angle)).astype(
                jnp.bfloat16
            )
        return carry

    lax.fori_loop(0, volume // tile, fill, 0)
    angle = shift_rows(volume, BOX)
    steer_ref[:, :volume] = jnp.cos(angle)
    steer_ref[:, volume:] = jnp.sin(angle)

    own_meta.wait()

    def wait_meta(k, carry):
        meta_copy(k).wait()
        return carry

    lax.fori_loop(1, peers, wait_meta, 0)
    to_smem = pltpu.make_async_copy(in_meta_ref, index_ref, local_sem)
    to_smem.start()
    to_smem.wait()
    own.wait()

    def spec_copy(c):
        slot = c % 2
        return pltpu.make_async_copy(
            stage.at[slot], spec_ref.at[pl.ds(c * n, n)], spec_sem.at[slot]
        )

    def one_chunk(c, carry):
        def fetch(i, carry):
            o = index_ref[i // each, 0, c * each + i % each]
            got[i] = refs_ref[o]
            return carry

        lax.fori_loop(0, n, fetch, 0)

        def wait_rows(k, carry):
            row_copy(c, k).wait()
            return carry

        lax.fori_loop(1, peers, wait_rows, 0)

        @pl.when(c >= 2)
        def _():
            spec_copy(c - 2).wait()

        flat = rows[c].reshape(n * planes, volume)
        slot = c % 2
        width = 256
        for at in range(0, volume, width):
            re = slice(at, at + width)
            im = slice(volume + at, volume + at + width)
            s_re = jnp.dot(flat, table[:, re], preferred_element_type=jnp.float32)
            s_im = jnp.dot(flat, table[:, im], preferred_element_type=jnp.float32)
            s_re = s_re.reshape(n, planes, width)
            s_im = s_im.reshape(n, planes, width)
            stage[slot, :, :, re] = s_re.astype(jnp.bfloat16)
            stage[slot, :, :, im] = s_im.astype(jnp.bfloat16)
            r_re = got[:, :, re].astype(jnp.float32)
            r_im = got[:, :, im].astype(jnp.float32)
            q[:, re] = jnp.sum(s_re * r_re + s_im * r_im, axis=1)
            q[:, im] = jnp.sum(s_im * r_re - s_re * r_im, axis=1)
        nt = (((1,), (1,)), ((), ()))
        every_ref[pl.ds(c * n, n), :] = (
            lax.dot_general(
                q[:, :volume], steer_ref[:, :volume], nt, precision=HIGH,
                preferred_element_type=jnp.float32,
            )
            - lax.dot_general(
                q[:, volume:], steer_ref[:, volume:], nt, precision=HIGH,
                preferred_element_type=jnp.float32,
            )
        ) * (1.0 / volume)
        spec_copy(c).start()
        return carry

    lax.fori_loop(0, chunks, one_chunk, 0)
    for c in range(max(chunks - 2, 0), chunks):
        spec_copy(c).wait()


def exchange(holder, particles, sent_meta, refs):
    chunks = CHUNKS
    peers = sent_meta.shape[0]
    n = holder.shape[0] // chunks
    each = n // peers
    planes, volume = particles.shape[1:]
    owned = refs.shape[0]
    return pl.pallas_call(
        functools.partial(exchange_kernel, peers),
        out_shape=(
            jax.ShapeDtypeStruct((chunks * n, planes, 2 * volume), jnp.bfloat16),
            jax.ShapeDtypeStruct((chunks * n, BINS), jnp.float32),
            jax.ShapeDtypeStruct(sent_meta.shape, jnp.int32),
            jax.ShapeDtypeStruct((BINS, 2 * volume), jnp.float32),
        ),
        in_specs=[SMEM_SPEC, VMEM_SPEC, VMEM_SPEC, VMEM_SPEC],
        out_specs=(ANY_SPEC, VMEM_SPEC, VMEM_SPEC, VMEM_SPEC),
        scratch_shapes=[
            pltpu.VMEM((chunks, peers, each, planes, volume), jnp.bfloat16),
            pltpu.VMEM((chunks, peers, each, planes, volume), jnp.bfloat16),
            pltpu.VMEM((volume, 2 * volume), jnp.bfloat16),
            pltpu.VMEM((n, planes, 2 * volume), jnp.bfloat16),
            pltpu.VMEM((n, 2 * volume), jnp.float32),
            pltpu.VMEM((2, n, planes, 2 * volume), jnp.bfloat16),
            pltpu.SMEM(sent_meta.shape, jnp.int32),
            pltpu.SemaphoreType.DMA((chunks, peers)),
            pltpu.SemaphoreType.DMA((chunks, peers)),
            pltpu.SemaphoreType.DMA,
            pltpu.SemaphoreType.DMA((peers,)),
            pltpu.SemaphoreType.DMA((peers,)),
            pltpu.SemaphoreType.DMA,
            pltpu.SemaphoreType.DMA((2,)),
        ],
        compiler_params=pltpu.CompilerParams(
            collective_id=0, has_side_effects=True, vmem_limit_bytes=48 * 2**20
        ),
    )(holder, particles, sent_meta, refs)


def add_kernel(
    local_ref, tilt_ref, binned_ref, mass_ref, steer_ref, wedge_ref, spec_ref, out_ref, sq_ref,
    fresh_ref, weight, phi, spec, sems, out_sems
):
    owned, planes, two = fresh_ref.shape
    volume = two // 2
    chunks, n = spec.shape[:2]

    def load(c):
        return pltpu.make_async_copy(spec_ref.at[pl.ds(c * n, n)], spec.at[c], sems.at[c])

    for c in range(chunks):
        load(c).start()
    phi[...] = jnp.dot(
        binned_ref[...], steer_ref[...], precision=HIGH, preferred_element_type=jnp.float32
    )

    def clear(o, carry):
        fresh_ref[o] = jnp.zeros((planes, two), jnp.float32)
        weight[o] = jnp.zeros((planes, volume), jnp.float32)
        return carry

    lax.fori_loop(0, owned, clear, 0, unroll=2)
    for c in range(chunks):
        load(c).wait()

        def add(j, carry, c=c):
            p = c * n + j
            o = local_ref[p]

            @pl.when(o >= 0)
            def _():
                wed = wedge_ref[tilt_ref[p]]
                row = pl.ds(p, 1)
                p_re = phi[row, :volume] * wed
                p_im = phi[row, volume:two] * wed
                s_re = spec[c, j, :, :volume].astype(jnp.float32)
                s_im = spec[c, j, :, volume:].astype(jnp.float32)
                fresh_ref[o, :, :volume] += p_re * s_re - p_im * s_im
                fresh_ref[o, :, volume:] += p_re * s_im + p_im * s_re
                weight[o] += mass_ref[p] * wed

            return carry

        lax.fori_loop(0, n, add, 0)

    def finish(o, carry):
        inv = 1.0 / (weight[o] + 1.0)
        a_re = fresh_ref[o, :, :volume] * inv
        a_im = fresh_ref[o, :, volume:] * inv
        fresh_ref[o, :, :volume] = a_re
        fresh_ref[o, :, volume:] = a_im
        total = a_re * a_re + a_im * a_im
        part = total[:, :128]
        for at in range(128, volume, 128):
            part = part + total[:, at : at + 128]
        sq_ref[o] = part
        return carry

    pieces = out_sems.shape[0]
    size = owned // pieces

    def store(i):
        return pltpu.make_async_copy(
            fresh_ref.at[pl.ds(i * size, size)], out_ref.at[pl.ds(i * size, size)], out_sems.at[i]
        )

    for i in range(pieces):
        lax.fori_loop(i * size, (i + 1) * size, finish, 0, unroll=2)
        store(i).start()
    for i in range(pieces):
        store(i).wait()


def accumulate(local, tilt, binned, mass, steerer, wedge, spec, owned):
    slots, planes, two = spec.shape
    volume = two // 2
    n = slots // CHUNKS
    return pl.pallas_call(
        add_kernel,
        out_shape=(
            jax.ShapeDtypeStruct((owned, planes, two), jnp.float32),
            jax.ShapeDtypeStruct((owned, planes, 128), jnp.float32),
        ),
        in_specs=[SMEM_SPEC, SMEM_SPEC, VMEM_SPEC, SMEM_SPEC, VMEM_SPEC, VMEM_SPEC, ANY_SPEC],
        out_specs=(ANY_SPEC, VMEM_SPEC),
        scratch_shapes=[
            pltpu.VMEM((owned, planes, two), jnp.float32),
            pltpu.VMEM((owned, planes, volume), jnp.float32),
            pltpu.VMEM((slots, two), jnp.float32),
            pltpu.VMEM((CHUNKS, n, planes, two), jnp.bfloat16),
            pltpu.SemaphoreType.DMA((CHUNKS,)),
            pltpu.SemaphoreType.DMA((8,)),
        ],
        compiler_params=pltpu.CompilerParams(vmem_limit_bytes=56 * 2**20),
        cost_estimate=pl.CostEstimate(
            flops=20 * slots * planes * volume, bytes_accessed=64 * 2**20, transcendentals=0
        ),
    )(local, tilt, binned, mass, steerer, wedge, spec)


def shards(particles, refs, orient, shifts, tilt, wedge):
    count, planes, volume = particles.shape
    owned = refs.shape[0]
    ncand = shifts.shape[1]
    peers = lax.axis_size("dom")
    capacity = 2 * count // peers
    slots_all = peers * capacity
    each = capacity // CHUNKS
    rows_chunk = peers * each

    owner = orient // owned
    index = jnp.arange(count, dtype=jnp.int32)
    same = (owner[:, None] == owner[None, :]) & (index[None, :] < index[:, None])
    rank = jnp.sum(same.astype(jnp.int32), axis=1)
    slot = (rank // each) * rows_chunk + owner * each + rank % each
    slot_hot = slot[None, :] == jnp.arange(slots_all, dtype=jnp.int32)[:, None]
    holder = jnp.sum(jnp.where(slot_hot, index[None, :], 0), axis=1)
    bins = (shifts[:, :, 0] + 4) * 9 + (shifts[:, :, 1] + 4)
    fields = [orient % owned, jnp.ones_like(orient), tilt] + [bins[:, k] for k in range(ncand)]
    height = -(-len(fields) // 8) * 8
    lanes = -(-capacity // 128) * 128
    meta = jnp.stack(fields + [jnp.zeros_like(orient)] * (height - len(fields)), axis=0)
    place_hot = rank[:, None] == jnp.arange(lanes, dtype=jnp.int32)[None, :]
    owner_hot = owner[None, :] == jnp.arange(peers, dtype=jnp.int32)[:, None]
    spread = (owner_hot[:, None, :] * meta[None, :, :]).astype(jnp.float32)
    sent_meta = jnp.dot(
        spread.reshape(peers * height, count), place_hot.astype(jnp.float32), precision=HIGH
    )
    sent_meta = jnp.round(sent_meta).astype(jnp.int32).reshape(peers, height, lanes)
    spec, every, in_meta, steerer = exchange(holder, particles, sent_meta, refs)
    in_meta = in_meta[:, : 3 + ncand, :capacity].reshape(peers, 3 + ncand, CHUNKS, each)
    in_meta = in_meta.transpose(1, 2, 0, 3).reshape(3 + ncand, slots_all)
    local = jnp.where(in_meta[1] > 0, in_meta[0], -1)
    work_tilt = in_meta[2]
    work_bins = in_meta[3:].T
    hot = (work_bins[:, :, None] == jnp.arange(BINS, dtype=jnp.int32)[None, None, :]).astype(
        jnp.float32
    )
    corr = jnp.sum(hot * every[:, None, :], axis=2)
    corr = jnp.sum(
        lax.all_gather(corr.T.reshape(-1, 128), "slab", axis=0, tiled=False), axis=0
    ).reshape(ncand, slots_all).T
    score = corr / math.sqrt(BOX)
    square = score * score
    weights = square / (4.0 + jnp.sum(square, axis=1, keepdims=True))
    binned = jnp.sum(hot * weights[:, :, None], axis=1)
    mass = jnp.sum(weights, axis=1)
    fresh, sq = accumulate(local, work_tilt, binned, mass, steerer, wedge, spec, owned)

    back = lax.all_to_all(
        weights.reshape(CHUNKS, peers, each * ncand).transpose(1, 0, 2).reshape(peers, -1),
        "dom",
        split_axis=0,
        concat_axis=0,
        tiled=True,
    )
    back = back.reshape(peers, CHUNKS, each, ncand).transpose(1, 0, 2, 3).reshape(slots_all, ncand)
    shift_weights = jnp.dot(slot_hot.T.astype(jnp.float32), back, precision=HIGH)

    sums = jnp.sum(sq, axis=(1, 2))
    sumsq = jnp.sum(lax.all_gather(sums, "slab", axis=0, tiled=False), axis=0)
    rms = jnp.sqrt(sumsq / (BOX * volume))
    new_refs = fresh / jnp.maximum(rms, 1.0)[:, None, None]
    return (new_refs, shift_weights)


def solution(mesh):
    placed = (
        P("dom", "slab", None),
        P("dom", "slab", None),
        P("dom"),
        P("dom", None, None),
        P("dom"),
        P(None, "slab", None),
    )
    return jax.shard_map(
        shards,
        mesh=mesh,
        in_specs=placed,
        out_specs=(P("dom", "slab", None), P("dom", None)),
        check_vma=False,
    )
```

profile of v0, /device:TPU:0, one launch (start us, length us, event | category | flops | bytes accessed | tf_op | source)
XLA Modules:
  0.0 219.7 jit_solution(7444874677216047275)
XLA Ops:
  0.6 0.7 and_select_fusion
  1.3 0.2 convert_reduce_fusion
  1.6 0.8 fusion.13
  2.5 0.7 stack.15
  3.3 0.3 fusion
  3.6 1.9 copy-done
  5.5 143.9 %shard_map.77 = (bf16[384,8,2048]{2,1,0:T(8,128)(2,1)}, f32[384,128]{1,0:T(8,128)S(1)}, s32[8,16,128]{2,1,0:T(8,128)S(1)}, f32[128,2048]{1,0:T(8,128)S(1)}) custom-call(s32[384]{0:T(512)S(1)} %select_reduce_fusion.2.holder_ref, bf16[192,8,1024]{2,1,0:T(8,128)(2,1)S(1)} %copy-done, s32[8,16,128]{2,1,0:T(8,128)S(1)} %bitcast.45, bf16[256,8,2048]{2,1,0:T(8,128)(2,1)} %refs_ref.1), custom_call_target="tpu_custom_call" | custom-call | tf_op jit(solution)/shard_map/pallas_call | solution.py:190
  149.4 1.0 copy-done.1
  151.1 1.2 select_reduce_fusion.1
  152.4 5.2 %all_gather.9 = f32[4,24,128]{2,1,0:T(8,128)S(1)} all-gather(f32[1,24,128]{2,1,0:T(8,128)S(1)} %all_gather_reshape.3), channel_id=1, replica_groups=mesh['dom'=8,'slab'=4] {'slab'}, dimensions={0}, use_global_device_ids=true | all-gather | bytes 61440 | tf_op jit(solution)/shard_map/all_gather | solution.py:363
  157.7 0.6 fusion.9
  158.6 0.7 all_to_all.8
  159.3 12.8 %all-to-all-start = ((f32[8,1,384]{2,1,0:T(1,128)}), f32[8,1,384]{2,1,0:T(1,128)S(1)}, u32[]{:S(2)}, u32[]{:S(2)}) async-start(f32[8,1,384]{2,1,0:T(1,128)} %all_to_all.8), calls=%async_computation | async-start | bytes 24576 | tf_op jit(solution)/shard_map/all_to_all | solution.py:372
  172.0 2.6 %select_reduce_fusion.binned_ref = f32[384,128]{1,0:T(8,128)} fusion(f32[384,8]{1,0:T(8,128)S(1)} %copy.40, s32[384,8]{1,0:T(8,128)S(1)} %copy.38), kind=kLoop, calls=%fused_computation.1 | loop fusion | flops 1130496 | bytes 221184 | tf_op jit(solution)/shard_map/reduce_sum | solution.py:368
  174.6 0.2 fusion.12
  174.8 0.3 copy.36
  175.1 0.7 squeeze.2.tilt_ref
  175.8 0.3 copy.35
  176.2 0.7 select_n.35.local_ref
  176.8 21.7 %shard_map.78 = (f32[256,8,2048]{2,1,0:T(8,128)}, f32[256,8,128]{2,1,0:T(8,128)}) custom-call(s32[384]{0:T(512)} %select_n.35.local_ref, s32[384]{0:T(512)} %squeeze.2.tilt_ref, f32[384,128]{1,0:T(8,128)} %select_reduce_fusion.binned_ref, f32[384]{0:T(512)} %get-tuple-element.18.mass_ref, f32[128,2048]{1,0:T(8,128)} %copy-done.1, f32[16,8,1024]{2,1,0:T(8,128)} %wedge_ref.1, ...), custom_call_target="tpu_custom_call" | custom-call | flops 62914560 | bytes 67108864 | tf_op jit(solution)/shard_map/pallas_call | solution.py:300
  198.5 2.3 %reduce_sum.88 = f32[256]{0:T(256)S(1)} reduce(f32[256,8,128]{2,1,0:T(8,128)} %get-tuple-element.13, f32[]{:T(128)} %constant.69.clone.1), dimensions={1,2}, to_apply=%region_7.8 | reduce | flops 261888 | bytes 1049604 | tf_op jit(solution)/shard_map/reduce_sum | solution.py:382
  200.8 5.1 %all-gather.1 = f32[4,1,256]{2,1,0:T(1,128)S(1)} all-gather(f32[1,1,256]{2,1,0:T(1,128)S(1)} %bitcast.54), channel_id=2, replica_groups=mesh['dom'=8,'slab'=4] {'slab'}, dimensions={0}, use_global_device_ids=true | all-gather | bytes 5120 | tf_op jit(solution)/shard_map/all_gather | solution.py:383
  205.9 12.4 %broadcast_divide_fusion = f32[256,8,2048]{2,1,0:T(8,128)} fusion(f32[256,8,2048]{2,1,0:T(8,128)} %get-tuple-element.12, f32[256]{0:T(256)S(1)} %sqrt_maximum_fusion), kind=kLoop, calls=%fused_computation | loop fusion | flops 4194304 | bytes 33555456 | tf_op jit(solution)/shard_map/div | solution.py:385
  218.7 0.9 fusion.1
  (33 shorter events, 1.7 us)
Async XLA Ops:
  3.6 1.9 copy-start
  149.4 1.1 copy-start.1
  159.3 59.0 %all-to-all-start = ((f32[8,1,384]{2,1,0:T(1,128)}), f32[8,1,384]{2,1,0:T(1,128)S(1)}, u32[]{:S(2)}, u32[]{:S(2)}) async-start(f32[8,1,384]{2,1,0:T(1,128)} %all_to_all.8), calls=%async_computation | async-start | bytes 24576 | tf_op jit(solution)/shard_map/all_to_all | solution.py:372
where the time goes:
time: 224 us; the launch traced here: 220 us
  Pallas kernels  166 us (74%)
  other arithmetic  20.3 us (9%)
  starting transfers between devices  12.8 us (6%)
  blocking collectives  10.3 us (5%)
  local copies, waits for them, and re-layouts  8.6 us (4%)
    pallas_call x1, Pallas kernels, exchange(): pl.pallas_call(functools.partial(exchange_kernel, peers), out_shape=(jax....  144 us
    pallas_call x1, Pallas kernels, accumulate(): pl.pallas_call(add_kernel, out_shape=(jax.ShapeDtypeStruct((owned, planes...  21.7 us
    all_to_all x1, starting transfers between devices, shards(): lax.all_to_all(weights.reshape(CHUNKS, peers, each * ncand).transpose(1,...  12.8 us
    div x1, other arithmetic, shards(): new_refs = fresh / jnp.maximum(rms, 1.0)[:, None, None]  12.4 us
    all_gather x1, blocking collectives, shards(): lax.all_gather(corr.T.reshape(-1, 128), 'slab', axis=0, tiled=False)  5.23 us
    all_gather x1, blocking collectives, shards(): sumsq = jnp.sum(lax.all_gather(sums, 'slab', axis=0, tiled=False), axis=0)  5.06 us
  transfers between devices with their start and end apart: 1, of which 0 were waited for; matrix products, arithmetic and copies ran while one was open for 9% of the time, Pallas kernels for 10%

commit v1 on v0

v1 whole, which is shorter than its diff:
```python
import functools
import math

import jax
import jax.numpy as jnp
from jax import lax
from jax.experimental import pallas as pl
from jax.experimental.pallas import tpu as pltpu
from jax.sharding import PartitionSpec as P

BOX = 32
CHUNKS = 12
BATCH = 6
GROUP = 16
BINS = 128
LANES = 128
WIDTH = 256
AHEAD = 2

MESH = pl.DeviceIdType.MESH
HIGH = lax.Precision.HIGHEST
VMEM_SPEC = pl.BlockSpec(memory_space=pltpu.VMEM)
SMEM_SPEC = pl.BlockSpec(memory_space=pltpu.SMEM)
ANY_SPEC = pl.BlockSpec(memory_space=pl.ANY)
NT = (((1,), (1,)), ((), ()))
TN = (((0,), (0,)), ((), ()))


def iota(shape, dim):
    return lax.broadcasted_iota(jnp.int32, shape, dim)


def angle_rows(phase, box):
    return (phase % box).astype(jnp.float32) * (2.0 * math.pi / box)


def step_kernel(
    peers, slabs, holder_ref, slot_ref, bins_ref, from_ref, meta_ref, refs_hbm, wedge_hbm,
    acc_ref, scale_ref, weights_ref,
    particles, out_ref, rows, table, refs_ref, wedge_ref, wedge3, got, stage, q, phi,
    mixed, contrib, masses, select, weight, steer, every, share, back_ref, picked,
    in_meta, meta_cols, cols, edge, part, sums, index_ref,
    load_sem, send, recv, meta_send, meta_recv, local_sem,
    ev_send, ev_recv, back_send, back_recv, sum_send, sum_recv,
):
    chunks, _, each, planes, volume = rows.shape
    n = peers * each
    rows_all, two = acc_ref.shape
    owned = rows_all // planes
    tilts = wedge_ref.shape[0]
    slots = BATCH * n
    count_all, ncand = weights_ref.shape
    me = lax.axis_index("dom")
    mine = lax.axis_index("slab")

    load_rows = pltpu.make_async_copy(from_ref, particles, load_sem.at[0])
    load_refs = pltpu.make_async_copy(refs_hbm, refs_ref, load_sem.at[1])
    load_wedge = pltpu.make_async_copy(wedge_hbm, wedge_ref, load_sem.at[2])
    load_rows.start()
    load_refs.start()
    load_wedge.start()

    barrier = pltpu.get_barrier_semaphore()
    for k in range(1, peers):
        pl.semaphore_signal(
            barrier, inc=1, device_id={"dom": lax.rem(me + k, peers)}, device_id_type=MESH
        )
    for k in range(1, slabs):
        pl.semaphore_signal(
            barrier, inc=1, device_id={"slab": lax.rem(mine + k, slabs)}, device_id_type=MESH
        )
    pl.semaphore_wait(barrier, peers - 1 + slabs - 1)

    def partner(k):
        return lax.rem(me + k, peers)

    def meta_copy(k):
        to = partner(k)
        return pltpu.make_async_remote_copy(
            src_ref=meta_ref.at[to], dst_ref=in_meta.at[me],
            send_sem=meta_send.at[k], recv_sem=meta_recv.at[k],
            device_id={"dom": to}, device_id_type=MESH,
        )

    def row_copy(c, k):
        to = partner(k)
        return pltpu.make_async_remote_copy(
            src_ref=out_ref.at[c, to], dst_ref=rows.at[c, me],
            send_sem=send.at[c, k], recv_sem=recv.at[c, k],
            device_id={"dom": to}, device_id_type=MESH,
        )

    def every_copy(c, k):
        return pltpu.make_async_remote_copy(
            src_ref=every.at[c, mine], dst_ref=every.at[c, mine],
            send_sem=ev_send.at[c, k], recv_sem=ev_recv.at[c, k],
            device_id={"slab": lax.rem(mine + k, slabs)}, device_id_type=MESH,
        )

    def back_copy(c, k):
        to = partner(k)
        return pltpu.make_async_remote_copy(
            src_ref=share.at[c, to], dst_ref=back_ref.at[c, me],
            send_sem=back_send.at[c, k], recv_sem=back_recv.at[c, k],
            device_id={"dom": to}, device_id_type=MESH,
        )

    def sum_copy(k):
        return pltpu.make_async_remote_copy(
            src_ref=sums.at[mine], dst_ref=sums.at[mine],
            send_sem=sum_send.at[k], recv_sem=sum_recv.at[k],
            device_id={"slab": lax.rem(mine + k, slabs)}, device_id_type=MESH,
        )

    def over(first, last, make, act):
        def body(k, carry):
            act(make(k))
            return carry

        lax.fori_loop(first, last, body, 0)

    over(1, peers, meta_copy, lambda x: x.start())
    load_rows.wait()

    def pick_chunk(c, carry):
        def pick_owner(k, carry):
            to = partner(k)
            for j in range(each):
                out_ref[c, to, j] = particles[holder_ref[c * n + to * each + j]]

            @pl.when(c < AHEAD)
            def _():
                row_copy(c, k).start()

            return carry

        lax.fori_loop(1, peers, pick_owner, 0)
        for j in range(each):
            rows[c, me, j] = particles[holder_ref[c * n + me * each + j]]
        return carry

    lax.fori_loop(0, chunks, pick_chunk, 0)
    in_meta[me] = meta_ref[me]

    at_y, ky = iota((BOX, volume), 0), iota((BOX, volume), 1) // BOX
    kx = iota((BOX, volume), 1) % BOX
    angle_y = angle_rows(at_y * ky, BOX)
    angle_x = angle_rows(at_y * kx, BOX)
    edge[0] = jnp.cos(angle_y)
    edge[1] = jnp.sin(angle_y)
    edge[2] = jnp.cos(angle_x)
    edge[3] = jnp.sin(angle_x)

    def fill(y, carry):
        at = pl.multiple_of(y * BOX, BOX)
        for j in range(0, volume, WIDTH):
            part_of = slice(j, j + WIDTH)
            cos_y, sin_y = edge[0, pl.ds(y, 1), part_of], edge[1, pl.ds(y, 1), part_of]
            cos_x, sin_x = edge[2, :, part_of], edge[3, :, part_of]
            table[pl.ds(at, BOX), part_of] = (cos_y * cos_x - sin_y * sin_x).astype(jnp.bfloat16)
            table[pl.ds(at, BOX), volume + j : volume + j + WIDTH] = (
                -(sin_y * cos_x + cos_y * sin_x)
            ).astype(jnp.bfloat16)
        return carry

    lax.fori_loop(0, BOX, fill, 0)

    def fill_steer(j, carry):
        at = pl.multiple_of(j * LANES, LANES)
        bins = iota((BINS, LANES), 0)
        freq = iota((BINS, LANES), 1) + at
        angle = angle_rows(
            (bins // 9 - 4) * (freq // BOX) + (bins % 9 - 4) * (freq % BOX) + 32 * BOX, BOX
        )
        steer[:, pl.ds(at, LANES)] = jnp.cos(angle)
        steer[:, pl.ds(pl.multiple_of(volume + at, LANES), LANES)] = jnp.sin(angle)
        return carry

    lax.fori_loop(0, volume // LANES, fill_steer, 0)

    def clear(i, carry):
        at = pl.multiple_of(i * 8, 8)
        acc_ref[pl.ds(at, 8), :] = jnp.zeros((8, two), jnp.float32)
        return carry

    lax.fori_loop(0, rows_all // 8, clear, 0)
    sums[mine] = jnp.zeros(sums.shape[1:], jnp.float32)

    weight[...] = jnp.zeros(weight.shape, jnp.float32)
    part[...] = jnp.zeros(part.shape, jnp.float32)

    load_wedge.wait()
    for k in range(volume // LANES):
        at = slice(k * LANES, (k + 1) * LANES)
        mixed[k, : tilts * planes, :] = wedge_ref[:, :, at].reshape(tilts * planes, LANES)
        for z in range(planes):
            flat_wedge = mixed[k, pl.ds(z, tilts, stride=planes), :]
            wedge_hi = flat_wedge.astype(jnp.bfloat16)
            wedge3[z, :tilts, at] = wedge_hi
            wedge3[z, tilts : 2 * tilts, at] = wedge_hi
            wedge3[z, 2 * tilts :, at] = (flat_wedge - wedge_hi.astype(jnp.float32)).astype(
                jnp.bfloat16
            )

    over(1, peers, meta_copy, lambda x: x.wait())
    to_smem = pltpu.make_async_copy(in_meta, index_ref, local_sem)
    to_smem.start()
    fields = in_meta.shape[1]
    eye = (iota((fields, LANES), 0) == iota((fields, LANES), 1)).astype(jnp.float32)

    def turn(k, carry):
        meta_cols[k] = lax.dot_general(
            in_meta[k].astype(jnp.float32), eye, TN, preferred_element_type=jnp.float32
        )
        return carry

    lax.fori_loop(0, peers, turn, 0)
    to_smem.wait()
    load_refs.wait()

    def transform(c):
        slot = c % 2

        def fetch(i, carry):
            o = index_ref[i // each, 0, c * each + i % each]
            got[i] = refs_ref[jnp.maximum(o - 1, 0)]
            return carry

        lax.fori_loop(0, n, fetch, 0)
        over(1, peers, lambda k: row_copy(c, k), lambda x: x.wait())

        def one_width(j, carry):
            at = pl.multiple_of(j * WIDTH, WIDTH)
            re = pl.ds(at, WIDTH)
            im = pl.ds(pl.multiple_of(volume + at, WIDTH), WIDTH)
            flat = rows[c].reshape(n * planes, volume)
            s_re = jnp.dot(flat, table[:, re], preferred_element_type=jnp.float32)
            s_im = jnp.dot(flat, table[:, im], preferred_element_type=jnp.float32)
            s_re = s_re.reshape(n, planes, WIDTH)
            s_im = s_im.reshape(n, planes, WIDTH)
            stage[slot, :, :, re] = s_re.astype(jnp.bfloat16)
            stage[slot, :, :, im] = s_im.astype(jnp.bfloat16)
            r_re = got[:, :, re].astype(jnp.float32)
            r_im = got[:, :, im].astype(jnp.float32)
            q[:, re] = jnp.sum(s_re * r_re + s_im * r_im, axis=1)
            q[:, im] = jnp.sum(s_im * r_re - s_re * r_im, axis=1)
            return carry

        lax.fori_loop(0, volume // WIDTH, one_width, 0)
        every[c, mine] = (
            lax.dot_general(
                q[:, :volume], steer[:, :volume], NT, precision=HIGH,
                preferred_element_type=jnp.float32,
            )
            - lax.dot_general(
                q[:, volume:], steer[:, volume:], NT, precision=HIGH,
                preferred_element_type=jnp.float32,
            )
        ) * (1.0 / volume)
        over(1, slabs, lambda k: every_copy(c, k), lambda x: x.start())

        @pl.when(c + AHEAD < chunks)
        def _():
            over(1, peers, lambda k: row_copy(c + AHEAD, k), lambda x: x.start())

    def gather_add(c):
        slot = c % 2

        def one_col(i, carry):
            cols[pl.ds(i, 1), :] = meta_cols[i // each, pl.ds(c * each + i % each, 1), :]
            return carry

        lax.fori_loop(0, n, one_col, 0)
        field = cols[...]
        lanes = iota((n, LANES), 1)
        lanes_f = lanes.astype(jnp.float32)
        count = jnp.zeros((n, LANES), jnp.float32)
        for k in range(ncand):
            count = count + jnp.where(field[:, 2 + k : 3 + k] == lanes_f, 1.0, 0.0)
        at_tilt = (lanes % tilts).astype(jnp.float32) == field[:, 1:2]

        over(1, slabs, lambda k: every_copy(c, k), lambda x: x.wait())
        score = every[c, 0]
        for k in range(1, slabs):
            score = score + every[c, k]
        score = score / math.sqrt(BOX)
        square = score * score
        total = jnp.sum(count * square, axis=1, keepdims=True)
        shared = square / (4.0 + total)
        for k in range(peers):
            share[c, k] = shared[k * each : (k + 1) * each]
        back_ref[c, me] = share[c, me]
        over(1, peers, lambda k: back_copy(c, k), lambda x: x.start())
        binned = count * shared
        mass = jnp.sum(binned, axis=1, keepdims=True)
        phi[...] = jnp.dot(binned, steer[...], precision=HIGH, preferred_element_type=jnp.float32)

        base = (c % BATCH) * n
        held = pl.ds(pl.multiple_of(base, n), n)
        mass_rows = jnp.where(at_tilt, mass, 0.0)
        mass_hi = mass_rows.astype(jnp.bfloat16)
        masses[held, :LANES] = mass_hi
        masses[held, LANES:] = (mass_rows - mass_hi.astype(jnp.float32)).astype(jnp.bfloat16)

        def one_group(g, carry):
            for i in range(GROUP):
                p = g * GROUP + i
                wed = wedge_ref[index_ref[p // each, 1, c * each + p % each]]
                p_re = phi[pl.ds(p, 1), :volume] * wed
                p_im = phi[pl.ds(p, 1), volume:] * wed
                s_re = stage[slot, p, :, :volume].astype(jnp.float32)
                s_im = stage[slot, p, :, volume:].astype(jnp.float32)
                c_re = p_re * s_re - p_im * s_im
                c_im = p_re * s_im + p_im * s_re
                tiles = volume // LANES
                row = slice(i * planes, (i + 1) * planes)
                for k in range(tiles):
                    at = slice(k * LANES, (k + 1) * LANES)
                    mixed[k, row, :] = c_re[:, at]
                    mixed[tiles + k, row, :] = c_im[:, at]

            to = pl.ds(pl.multiple_of(base + g * GROUP, GROUP), GROUP)
            for z in range(planes):
                for k in range(two // LANES):
                    contrib[z, to, k * LANES : (k + 1) * LANES] = mixed[
                        k, pl.ds(z, GROUP, stride=planes), :
                    ].astype(jnp.bfloat16)
            return carry

        lax.fori_loop(0, n // GROUP, one_group, 0)

    def accumulate(b):
        lane = iota((LANES, slots), 1)
        place = (b * BATCH + lane // n) * each + lane % each
        targets = jnp.dot(
            in_meta[:, 0, :].astype(jnp.float32),
            (iota((LANES, slots), 0) == place).astype(jnp.float32),
            preferred_element_type=jnp.float32,
        )
        own = iota((peers, slots), 0) == (iota((peers, slots), 1) % n) // each
        target = jnp.sum(jnp.where(own, targets, 0.0), axis=0, keepdims=True) - 1.0
        row = iota((owned, slots), 0).astype(jnp.float32)
        select[...] = jnp.where(row == target, 1.0, 0.0).astype(jnp.bfloat16)

        def one_plane(z, carry):
            to = pl.ds(pl.multiple_of(z * owned, owned), owned)
            chosen = select[...]

            def one_width(j, carry):
                at = pl.ds(pl.multiple_of(j * WIDTH, WIDTH), WIDTH)
                acc_ref[to, at] += jnp.dot(
                    chosen, contrib[z, :, at], preferred_element_type=jnp.float32
                )
                return carry

            lax.fori_loop(0, two // WIDTH, one_width, 0)
            return carry

        lax.fori_loop(0, planes, one_plane, 0)
        weight[...] += jnp.dot(select[...], masses[...], preferred_element_type=jnp.float32)

    def one_chunk(c, carry):
        @pl.when(c < chunks)
        def _():
            transform(c)

        @pl.when(c >= 1)
        def _():
            gather_add(c - 1)

        @pl.when((c >= 1) & (c % BATCH == 0))
        def _():
            accumulate(c // BATCH - 1)

        return carry

    lax.fori_loop(0, chunks + 1, one_chunk, 0)

    group = min(64, owned)
    blocks = owned // group
    mass = weight[:, :LANES] + weight[:, LANES:]
    mass_hi = mass.astype(jnp.bfloat16).astype(jnp.float32)
    low = iota((owned, LANES), 1) // tilts == 1
    select_mass = jnp.where(low, mass - mass_hi, mass_hi)
    weight[:, :LANES] = select_mass

    def finish(i, carry):
        z, at_row = i // blocks, pl.multiple_of(i % blocks * group, group)
        row = pl.ds(pl.multiple_of(z * owned + at_row, group), group)
        lhs = weight[pl.ds(at_row, group), : 3 * tilts].astype(jnp.bfloat16)
        folded = part[pl.ds(at_row, group), :]
        for at in range(0, volume, WIDTH):
            re = slice(at, at + WIDTH)
            im = slice(volume + at, volume + at + WIDTH)
            inv = 1.0 / (
                jnp.dot(lhs, wedge3[z, :, re], preferred_element_type=jnp.float32) + 1.0
            )
            a_re = acc_ref[row, re] * inv
            a_im = acc_ref[row, im] * inv
            acc_ref[row, re] = a_re
            acc_ref[row, im] = a_im
            total = a_re * a_re + a_im * a_im
            for k in range(0, WIDTH, LANES):
                folded = folded + total[:, k : k + LANES]
        part[pl.ds(at_row, group), :] = folded
        return carry

    lax.fori_loop(0, planes * blocks, finish, 0)
    held_rows = [min(LANES, owned - g * LANES) for g in range(-(-owned // LANES))]
    for g, held in enumerate(held_rows):
        whole = jnp.dot(
            part[g * LANES : g * LANES + held, :], jnp.ones((LANES, LANES), jnp.float32),
            precision=HIGH, preferred_element_type=jnp.float32,
        )
        keep = iota((held, LANES), 0) == iota((held, LANES), 1)
        sums[mine, g : g + 1, :] = jnp.sum(jnp.where(keep, whole, 0.0), axis=0, keepdims=True)
    over(1, slabs, sum_copy, lambda x: x.start())

    def wait_back(c, carry):
        over(1, peers, lambda k: back_copy(c, k), lambda x: x.wait())
        return carry

    lax.fori_loop(0, chunks, wait_back, 0)

    def pick(p, carry):
        at = slot_ref[p]
        picked[pl.ds(p, 1), :] = back_ref[
            at // n, (at % n) // each, pl.ds(at % each, 1), :
        ]
        return carry

    lax.fori_loop(0, count_all, pick, 0, unroll=4)
    block = min(64, count_all)
    for at in range(0, count_all, block):
        lanes = iota((block, BINS), 1)
        held_at = picked[at : at + block, :]
        wanted = bins_ref[at : at + block, :]
        weights_ref[at : at + block, :] = jnp.concatenate(
            [
                jnp.sum(
                    jnp.where(lanes == wanted[:, k : k + 1], held_at, 0.0), axis=1, keepdims=True
                )
                for k in range(ncand)
            ],
            axis=1,
        )

    over(1, slabs, sum_copy, lambda x: x.wait())
    total = sums[0]
    for k in range(1, slabs):
        total = total + sums[k]
    rms = jnp.sqrt(total / (BOX * volume))
    scale = 1.0 / jnp.maximum(rms, 1.0)
    for g, held in enumerate(held_rows):
        keep = iota((held, LANES), 0) == iota((held, LANES), 1)
        column = jnp.sum(jnp.where(keep, scale[g : g + 1, :], 0.0), axis=1, keepdims=True)
        scale_ref[g * LANES : g * LANES + held, :] = jnp.broadcast_to(column, (held, LANES))


def refine(holder, slot, bins, particles, sent_meta, refs, wedge, slabs):
    chunks = CHUNKS
    peers, fields, _ = sent_meta.shape
    n = holder.shape[0] // chunks
    each = n // peers
    planes, volume = particles.shape[1:]
    owned = refs.shape[0]
    two = 2 * volume
    tilts = wedge.shape[0]
    bf16, f32 = jnp.bfloat16, jnp.float32
    dma = pltpu.SemaphoreType.DMA
    return pl.pallas_call(
        functools.partial(step_kernel, peers, slabs),
        out_shape=(
            pltpu.VMEM((owned * planes, two), f32),
            pltpu.VMEM((owned, LANES), f32),
            jax.ShapeDtypeStruct(bins.shape, f32),
        ),
        in_specs=[SMEM_SPEC, SMEM_SPEC, VMEM_SPEC, ANY_SPEC, VMEM_SPEC, ANY_SPEC, ANY_SPEC],
        out_specs=(VMEM_SPEC, VMEM_SPEC, VMEM_SPEC),
        scratch_shapes=[
            pltpu.VMEM(particles.shape, bf16),
            pltpu.VMEM((chunks, peers, each, planes, volume), bf16),
            pltpu.VMEM((chunks, peers, each, planes, volume), bf16),
            pltpu.VMEM((volume, two), bf16),
            pltpu.VMEM(refs.shape, bf16),
            pltpu.VMEM(wedge.shape, f32),
            pltpu.VMEM((planes, 3 * tilts, volume), bf16),
            pltpu.VMEM((n, planes, two), bf16),
            pltpu.VMEM((2, n, planes, two), bf16),
            pltpu.VMEM((n, two), f32),
            pltpu.VMEM((n, two), f32),
            pltpu.VMEM((two // LANES, max(GROUP, tilts) * planes, LANES), f32),
            pltpu.VMEM((planes, BATCH * n, two), bf16),
            pltpu.VMEM((BATCH * n, 2 * LANES), bf16),
            pltpu.VMEM((owned, BATCH * n), bf16),
            pltpu.VMEM((owned, 2 * LANES), f32),
            pltpu.VMEM((BINS, two), f32),
            pltpu.VMEM((chunks, slabs, n, BINS), f32),
            pltpu.VMEM((chunks, peers, each, BINS), f32),
            pltpu.VMEM((chunks, peers, each, BINS), f32),
            pltpu.VMEM((bins.shape[0], BINS), f32),
            pltpu.VMEM(sent_meta.shape, jnp.int32),
            pltpu.VMEM((peers, LANES, LANES), f32),
            pltpu.VMEM((n, LANES), f32),
            pltpu.VMEM((4, BOX, volume), f32),
            pltpu.VMEM((owned, LANES), f32),
            pltpu.VMEM((slabs, 8, LANES), f32),
            pltpu.SMEM(sent_meta.shape, jnp.int32),
            dma((3,)),
            dma((chunks, peers)),
            dma((chunks, peers)),
            dma((peers,)),
            dma((peers,)),
            dma,
            dma((chunks, slabs)),
            dma((chunks, slabs)),
            dma((chunks, peers)),
            dma((chunks, peers)),
            dma((slabs,)),
            dma((slabs,)),
        ],
        compiler_params=pltpu.CompilerParams(
            collective_id=0, has_side_effects=True, vmem_limit_bytes=47 * 2**20
        ),
        cost_estimate=pl.CostEstimate(
            flops=10**11, bytes_accessed=64 * 2**20, transcendentals=0
        ),
    )(holder, slot, bins, particles, sent_meta, refs, wedge)


def write_kernel(scale_ref, fresh_ref, out_ref, stage, sems):
    rows_all, two = out_ref.shape
    owned = scale_ref.shape[0]
    planes = rows_all // owned
    slots, tiles, size_rows = stage.shape[:3]
    size = size_rows // planes
    pieces = owned // size

    def store(i, k):
        row = pl.ds(pl.multiple_of(i * size_rows, size_rows), size_rows)
        return pltpu.make_async_copy(
            stage.at[i % slots, k],
            out_ref.at[row, pl.ds(k * LANES, LANES)],
            sems.at[i % slots, k],
        )

    def drain(i, carry):
        for k in range(tiles):
            store(i, k).wait()
        return carry

    def one_piece(i, carry):
        @pl.when(i >= slots)
        def _():
            drain(i - slots, 0)

        for at in range(0, size, 8):
            first = pl.multiple_of(i * size + at, 8)
            scale = scale_ref[pl.ds(first, 8), :]
            for z in range(planes):
                row = pl.ds(pl.multiple_of(z * owned + first, 8), 8)
                to = pl.ds(at * planes + z, 8, stride=planes)
                for k in range(tiles):
                    stage[i % slots, k, to, :] = (
                        fresh_ref[row, k * LANES : (k + 1) * LANES] * scale
                    )
        for k in range(tiles):
            store(i, k).start()
        return carry

    lax.fori_loop(0, pieces, one_piece, 0)
    lax.fori_loop(max(pieces - slots, 0), pieces, drain, 0)


def write(scale, fresh):
    rows_all, two = fresh.shape
    owned = scale.shape[0]
    size = min(16, owned)
    scale, fresh = (pltpu.with_memory_space_constraint(x, pltpu.VMEM) for x in (scale, fresh))
    return pl.pallas_call(
        write_kernel,
        out_shape=jax.ShapeDtypeStruct(fresh.shape, jnp.float32),
        in_specs=[VMEM_SPEC, VMEM_SPEC],
        out_specs=ANY_SPEC,
        scratch_shapes=[
            pltpu.VMEM((4, two // LANES, size * (rows_all // owned), LANES), jnp.float32),
            pltpu.SemaphoreType.DMA((4, two // LANES)),
        ],
        compiler_params=pltpu.CompilerParams(vmem_limit_bytes=24 * 2**20),
    )(scale, fresh)


def shards(particles, refs, orient, shifts, tilt, wedge):
    count, planes, volume = particles.shape
    owned = refs.shape[0]
    ncand = shifts.shape[1]
    peers = lax.axis_size("dom")
    slabs = lax.axis_size("slab")
    capacity = 2 * count // peers
    slots_all = peers * capacity
    each = capacity // CHUNKS
    rows_chunk = peers * each

    owner = orient // owned
    index = jnp.arange(count, dtype=jnp.int32)
    same = (owner[:, None] == owner[None, :]) & (index[None, :] < index[:, None])
    rank = jnp.sum(same.astype(jnp.int32), axis=1)
    slot = (rank // each) * rows_chunk + owner * each + rank % each
    slot_hot = slot[None, :] == jnp.arange(slots_all, dtype=jnp.int32)[:, None]
    holder = jnp.sum(jnp.where(slot_hot, index[None, :], 0), axis=1)
    bins = (shifts[:, :, 0] + 4) * 9 + (shifts[:, :, 1] + 4)
    fields = [orient % owned + 1, tilt] + [bins[:, k] for k in range(ncand)]
    height = -(-len(fields) // 8) * 8
    meta = jnp.stack(fields + [jnp.zeros_like(orient)] * (height - len(fields)), axis=0)
    place_hot = rank[:, None] == jnp.arange(LANES, dtype=jnp.int32)[None, :]
    owner_hot = owner[None, :] == jnp.arange(peers, dtype=jnp.int32)[:, None]
    spread = (owner_hot[:, None, :] * meta[None, :, :]).astype(jnp.float32)
    sent_meta = jnp.dot(
        spread.reshape(peers * height, count), place_hot.astype(jnp.float32), precision=HIGH
    )
    sent_meta = jnp.round(sent_meta).astype(jnp.int32).reshape(peers, height, LANES)
    fresh, scale, shift_weights = refine(
        holder, slot, bins, particles, sent_meta, refs,
        wedge, slabs,
    )
    new_refs = write(scale, fresh).reshape(owned, planes, 2 * volume)
    return (new_refs, shift_weights)


def solution(mesh):
    placed = (
        P("dom", "slab", None),
        P("dom", "slab", None),
        P("dom"),
        P("dom", None, None),
        P("dom"),
        P(None, "slab", None),
    )
    return jax.shard_map(
        shards,
        mesh=mesh,
        in_specs=placed,
        out_specs=(P("dom", "slab", None), P("dom", None)),
        check_vma=False,
    )
```

time: 224 us -> 203 us (0.906); the launches traced: 220 us -> 203 us
  Pallas kernels: 166 us -> 196 us
  other arithmetic: 20.3 us -> 1.6 us
  starting transfers between devices: 12.8 us -> 0 us
  blocking collectives: 10.3 us -> 0 us
  local copies, waits for them, and re-layouts: 8.6 us -> 2.91 us
    pallas_call x2, Pallas kernels: 166 us -> 196 us  [the longest x1 190 us: refine(): pl.pallas_call(functools.partial(step_kernel, peers, slabs), out_shape=(p...]
    all_to_all x1 -> x0, starting transfers between devices: 12.8 us -> none  [shards(): lax.all_to_all(weights.reshape(CHUNKS, peers, each * ncand).transpose(1,...]
    div x1 -> x0, other arithmetic: 12.4 us -> none  [shards(): new_refs = fresh / jnp.maximum(rms, 1.0)[:, None, None]]
    all_gather x2 -> x0, blocking collectives: 10.3 us -> none  [the longest x1 5.23 us: shards(): lax.all_gather(corr.T.reshape(-1, 128), 'slab', axis=0, tiled=False)]
    reduce_sum x7 -> x0, other arithmetic: 6.7 us -> none  [the longest x1 2.56 us: shards(): binned = jnp.sum(hot * weights[:, :, None], axis=1)]
    unnamed x4 -> x7, local copies, waits for them, and re-layouts: 2.93 us -> 0.68 us
  transfers between devices with their start and end apart: 1 -> 0, of which waited for: 0 -> 0; matrix products, arithmetic and copies ran while one was open for 9% -> 0% of each run, Pallas kernels for 10% -> 0%
where the time goes in v1:
time: 203 us
  Pallas kernels  196 us (97%)
  local copies, waits for them, and re-layouts  2.91 us (1%)
    pallas_call x1, Pallas kernels, refine(): pl.pallas_call(functools.partial(step_kernel, peers, slabs), out_shape=(p...  190 us
    pallas_call x1, Pallas kernels, write(): pl.pallas_call(write_kernel, out_shape=jax.ShapeDtypeStruct(fresh.shape,...  6.59 us

profile of v1, /device:TPU:0, one launch (start us, length us, event | category | flops | bytes accessed | tf_op | source)
XLA Modules:
  0.0 202.6 jit_solution(5244268027682906020)
XLA Ops:
  0.6 0.7 fusion.7
  1.3 0.2 convert_reduce_fusion
  1.5 0.0 copy-start.2
  1.5 0.7 select_reduce_fusion.holder_ref
  2.2 0.8 fusion.8
  3.1 0.1 copy.28
  3.2 0.0 copy-start
  3.2 0.6 slice_reduce_fusion
  3.8 0.7 stack.19
  4.5 0.9 fusion
  5.4 0.0 copy-done.2
  5.4 0.0 copy-done
  5.4 189.8 %shard_map.77 = (f32[2048,2048]{1,0:T(8,128)S(1)}, f32[256,128]{1,0:T(8,128)S(1)}, f32[192,8]{1,0:T(8,128)}) custom-call(s32[384]{0:T(512)} %select_reduce_fusion.holder_ref, s32[192]{0:T(256)} %copy-done.2, s32[192,8]{1,0:T(8,128)} %bitcast.17, bf16[192,8,1024]{2,1,0:T(8,128)(2,1)} %from_ref.1, s32[8,16,128]{2,1,0:T(8,128)} %bitcast.19, ...), custom_call_target="tpu_custom_call" | custom-call | flops 99999997952 | bytes 67108864 | tf_op jit(solution)/shard_map/pallas_call | solution.py:471
  195.3 0.0 copy-start.1
  195.3 6.6 %shard_map.78 = f32[2048,2048]{1,0:T(8,128)} custom-call(f32[256,128]{1,0:T(8,128)S(1)} %get-tuple-element.5.scale_ref, f32[2048,2048]{1,0:T(8,128)S(1)} %get-tuple-element.6.fresh_ref), custom_call_target="tpu_custom_call" | custom-call | tf_op jit(solution)/shard_map/pallas_call | solution.py:580
  201.9 0.0 copy-done.1
  201.9 0.7 copy.29
  (6 shorter events, 0.0 us)
Async XLA Ops:
  1.5 3.9 %copy-start.2 = (s32[192]{0:T(256)}, s32[192]{0:T(256)S(1)}, u32[]{:S(2)}) copy-start(s32[192]{0:T(256)S(1)} %fusion.6.slot_ref) | copy-start | bytes 2308
  3.2 2.3 %copy-start = (s32[192,8,1]{1,0,2:T(8,128)}, s32[192,8,1]{1,0,2:T(8,128)S(1)}, u32[]{:S(2)}) copy-start(s32[192,8,1]{1,0,2:T(8,128)S(1)} %copy.28) | copy-start | bytes 18436
  195.3 6.6 %copy-start.1 = (f32[192,8]{1,0:T(8,128)S(1)}, f32[192,8]{1,0:T(8,128)}, u32[]{:S(2)}) copy-start(f32[192,8]{1,0:T(8,128)} %get-tuple-element.15) | copy-start | bytes 18436

commit v2 on v1

--- a/solution.py
+++ b/solution.py
@@ -11,7 +11,6 @@
 BOX = 32
 CHUNKS = 12
 BATCH = 6
-GROUP = 16
 BINS = 128
 LANES = 128
 WIDTH = 256
@@ -34,11 +33,16 @@
     return (phase % box).astype(jnp.float32) * (2.0 * math.pi / box)
 
 
+def split(value):
+    high = value.astype(jnp.bfloat16)
+    return high, (value - high.astype(jnp.float32)).astype(jnp.bfloat16)
+
+
 def step_kernel(
     peers, slabs, holder_ref, slot_ref, bins_ref, from_ref, meta_ref, refs_hbm, wedge_hbm,
     acc_ref, scale_ref, weights_ref,
     particles, out_ref, rows, table, refs_ref, wedge_ref, wedge3, got, stage, q, phi,
-    mixed, contrib, masses, select, weight, steer, every, share, back_ref, picked,
+    mixed, turn_rows, wedge_tile, contrib, masses, select, weight, steer_hi, steer_lo, every, share, back_ref, picked,
     in_meta, meta_cols, cols, edge, part, sums, index_ref,
     load_sem, send, recv, meta_send, meta_recv, local_sem,
     ev_send, ev_recv, back_send, back_recv, sum_send, sum_recv,
@@ -172,8 +176,11 @@
         angle = angle_rows(
             (bins // 9 - 4) * (freq // BOX) + (bins % 9 - 4) * (freq % BOX) + 32 * BOX, BOX
         )
-        steer[:, pl.ds(at, LANES)] = jnp.cos(angle)
-        steer[:, pl.ds(pl.multiple_of(volume + at, LANES), LANES)] = jnp.sin(angle)
+        for value, to in ((jnp.cos(angle), at), (jnp.sin(angle), volume + at)):
+            to = pl.ds(pl.multiple_of(to, LANES), LANES)
+            high = value.astype(jnp.bfloat16)
+            steer_hi[:, to] = high
+            steer_lo[:, to] = (value - high.astype(jnp.float32)).astype(jnp.bfloat16)
         return carry
 
     lax.fori_loop(0, volume // LANES, fill_steer, 0)
@@ -192,15 +199,19 @@
     load_wedge.wait()
     for k in range(volume // LANES):
         at = slice(k * LANES, (k + 1) * LANES)
-        mixed[k, : tilts * planes, :] = wedge_ref[:, :, at].reshape(tilts * planes, LANES)
+        wedge_tile[...] = wedge_ref[:, :, at].reshape(tilts * planes, LANES)
         for z in range(planes):
-            flat_wedge = mixed[k, pl.ds(z, tilts, stride=planes), :]
+            flat_wedge = wedge_tile[pl.ds(z, tilts, stride=planes), :]
             wedge_hi = flat_wedge.astype(jnp.bfloat16)
             wedge3[z, :tilts, at] = wedge_hi
             wedge3[z, tilts : 2 * tilts, at] = wedge_hi
             wedge3[z, 2 * tilts :, at] = (flat_wedge - wedge_hi.astype(jnp.float32)).astype(
                 jnp.bfloat16
             )
+    to_row = iota(turn_rows.shape, 0)
+    turn_rows[...] = jnp.where(
+        iota(turn_rows.shape, 1) == to_row % n * planes + to_row // n, 1.0, 0.0
+    ).astype(jnp.bfloat16)
 
     over(1, peers, meta_copy, lambda x: x.wait())
     to_smem = pltpu.make_async_copy(in_meta, index_ref, local_sem)
@@ -226,7 +237,7 @@
             got[i] = refs_ref[jnp.maximum(o - 1, 0)]
             return carry
 
-        lax.fori_loop(0, n, fetch, 0)
+        lax.fori_loop(0, n, fetch, 0, unroll=4)
         over(1, peers, lambda k: row_copy(c, k), lambda x: x.wait())
 
         def one_width(j, carry):
@@ -243,19 +254,15 @@
             r_re = got[:, :, re].astype(jnp.float32)
             r_im = got[:, :, im].astype(jnp.float32)
             q[:, re] = jnp.sum(s_re * r_re + s_im * r_im, axis=1)
-            q[:, im] = jnp.sum(s_im * r_re - s_re * r_im, axis=1)
-            return carry
-
-        lax.fori_loop(0, volume // WIDTH, one_width, 0)
+            q[:, im] = jnp.sum(s_re * r_im - s_im * r_re, axis=1)
+            return carry
+
+        lax.fori_loop(0, volume // WIDTH, one_width, 0, unroll=True)
+        q_hi, q_lo = split(q[...])
         every[c, mine] = (
-            lax.dot_general(
-                q[:, :volume], steer[:, :volume], NT, precision=HIGH,
-                preferred_element_type=jnp.float32,
-            )
-            - lax.dot_general(
-                q[:, volume:], steer[:, volume:], NT, precision=HIGH,
-                preferred_element_type=jnp.float32,
-            )
+            lax.dot_general(q_hi, steer_hi[...], NT, preferred_element_type=jnp.float32)
+            + lax.dot_general(q_lo, steer_hi[...], NT, preferred_element_type=jnp.float32)
+            + lax.dot_general(q_hi, steer_lo[...], NT, preferred_element_type=jnp.float32)
         ) * (1.0 / volume)
         over(1, slabs, lambda k: every_copy(c, k), lambda x: x.start())
 
@@ -270,7 +277,7 @@
             cols[pl.ds(i, 1), :] = meta_cols[i // each, pl.ds(c * each + i % each, 1), :]
             return carry
 
-        lax.fori_loop(0, n, one_col, 0)
+        lax.fori_loop(0, n, one_col, 0, unroll=8)
         field = cols[...]
         lanes = iota((n, LANES), 1)
         lanes_f = lanes.astype(jnp.float32)
@@ -293,7 +300,12 @@
         over(1, peers, lambda k: back_copy(c, k), lambda x: x.start())
         binned = count * shared
         mass = jnp.sum(binned, axis=1, keepdims=True)
-        phi[...] = jnp.dot(binned, steer[...], precision=HIGH, preferred_element_type=jnp.float32)
+        binned_hi, binned_lo = split(binned)
+        phi[...] = (
+            jnp.dot(binned_hi, steer_hi[...], preferred_element_type=jnp.float32)
+            + jnp.dot(binned_lo, steer_hi[...], preferred_element_type=jnp.float32)
+            + jnp.dot(binned_hi, steer_lo[...], preferred_element_type=jnp.float32)
+        )
 
         base = (c % BATCH) * n
         held = pl.ds(pl.multiple_of(base, n), n)
@@ -302,32 +314,40 @@
         masses[held, :LANES] = mass_hi
         masses[held, LANES:] = (mass_rows - mass_hi.astype(jnp.float32)).astype(jnp.bfloat16)
 
-        def one_group(g, carry):
-            for i in range(GROUP):
-                p = g * GROUP + i
+        step = 16 // planes
+
+        def one_step(i, carry):
+            both = []
+            for j in range(step):
+                p = i * step + j
                 wed = wedge_ref[index_ref[p // each, 1, c * each + p % each]]
-                p_re = phi[pl.ds(p, 1), :volume] * wed
-                p_im = phi[pl.ds(p, 1), volume:] * wed
-                s_re = stage[slot, p, :, :volume].astype(jnp.float32)
-                s_im = stage[slot, p, :, volume:].astype(jnp.float32)
-                c_re = p_re * s_re - p_im * s_im
-                c_im = p_re * s_im + p_im * s_re
-                tiles = volume // LANES
-                row = slice(i * planes, (i + 1) * planes)
-                for k in range(tiles):
-                    at = slice(k * LANES, (k + 1) * LANES)
-                    mixed[k, row, :] = c_re[:, at]
-                    mixed[tiles + k, row, :] = c_im[:, at]
-
-            to = pl.ds(pl.multiple_of(base + g * GROUP, GROUP), GROUP)
+                both.append((phi[pl.ds(p, 1), :volume] * wed, phi[pl.ds(p, 1), volume:] * wed))
+            p_re = jnp.concatenate([x[0] for x in both], axis=0)
+            p_im = jnp.concatenate([x[1] for x in both], axis=0)
+            s_re, s_im = (
+                jnp.concatenate(
+                    [stage[slot, i * step + j, :, at].astype(jnp.float32) for j in range(step)],
+                    axis=0,
+                )
+                for at in (slice(0, volume), slice(volume, two))
+            )
+            row = pl.ds(pl.multiple_of(i * 16, 16), 16)
+            mixed[row, :volume] = (p_re * s_re - p_im * s_im).astype(jnp.bfloat16)
+            mixed[row, volume:] = (p_re * s_im + p_im * s_re).astype(jnp.bfloat16)
+            return carry
+
+        lax.fori_loop(0, n // step, one_step, 0, unroll=2)
+
+        def one_turn(j, carry):
+            at = pl.ds(pl.multiple_of(j * WIDTH, WIDTH), WIDTH)
+            turned = jnp.dot(
+                turn_rows[...], mixed[:, at], preferred_element_type=jnp.float32
+            ).astype(jnp.bfloat16)
             for z in range(planes):
-                for k in range(two // LANES):
-                    contrib[z, to, k * LANES : (k + 1) * LANES] = mixed[
-                        k, pl.ds(z, GROUP, stride=planes), :
-                    ].astype(jnp.bfloat16)
-            return carry
-
-        lax.fori_loop(0, n // GROUP, one_group, 0)
+                contrib[z, held, at] = turned[z * n : (z + 1) * n]
+            return carry
+
+        lax.fori_loop(0, two // WIDTH, one_turn, 0, unroll=True)
 
     def accumulate(b):
         lane = iota((LANES, slots), 1)
@@ -353,10 +373,10 @@
                 )
                 return carry
 
-            lax.fori_loop(0, two // WIDTH, one_width, 0)
-            return carry
-
-        lax.fori_loop(0, planes, one_plane, 0)
+            lax.fori_loop(0, two // WIDTH, one_width, 0, unroll=True)
+            return carry
+
+        lax.fori_loop(0, planes, one_plane, 0, unroll=2)
         weight[...] += jnp.dot(select[...], masses[...], preferred_element_type=jnp.float32)
 
     def one_chunk(c, carry):
@@ -405,7 +425,7 @@
         part[pl.ds(at_row, group), :] = folded
         return carry
 
-    lax.fori_loop(0, planes * blocks, finish, 0)
+    lax.fori_loop(0, planes * blocks, finish, 0, unroll=4)
     held_rows = [min(LANES, owned - g * LANES) for g in range(-(-owned // LANES))]
     for g, held in enumerate(held_rows):
         whole = jnp.dot(
@@ -429,7 +449,7 @@
         ]
         return carry
 
-    lax.fori_loop(0, count_all, pick, 0, unroll=4)
+    lax.fori_loop(0, count_all, pick, 0, unroll=8)
     block = min(64, count_all)
     for at in range(0, count_all, block):
         lanes = iota((block, BINS), 1)
@@ -489,12 +509,15 @@
             pltpu.VMEM((2, n, planes, two), bf16),
             pltpu.VMEM((n, two), f32),
             pltpu.VMEM((n, two), f32),
-            pltpu.VMEM((two // LANES, max(GROUP, tilts) * planes, LANES), f32),
+            pltpu.VMEM((n * planes, two), bf16),
+            pltpu.VMEM((n * planes, n * planes), bf16),
+            pltpu.VMEM((tilts * planes, LANES), f32),
             pltpu.VMEM((planes, BATCH * n, two), bf16),
             pltpu.VMEM((BATCH * n, 2 * LANES), bf16),
             pltpu.VMEM((owned, BATCH * n), bf16),
             pltpu.VMEM((owned, 2 * LANES), f32),
-            pltpu.VMEM((BINS, two), f32),
+            pltpu.VMEM((BINS, two), bf16),
+            pltpu.VMEM((BINS, two), bf16),
             pltpu.VMEM((chunks, slabs, n, BINS), f32),
             pltpu.VMEM((chunks, peers, each, BINS), f32),
             pltpu.VMEM((chunks, peers, each, BINS), f32),

time: 203 us -> 186 us (0.916)
  Pallas kernels: 196 us -> 178 us
    pallas_call x1, Pallas kernels: 190 us -> 171 us  [refine(): pl.pallas_call(functools.partial(step_kernel, peers, slabs), out_shape=(p...]
where the time goes in v2:
time: 186 us; the launch traced here: 184 us
  Pallas kernels  178 us (96%)
  local copies, waits for them, and re-layouts  2.91 us (2%)
    pallas_call x1, Pallas kernels, refine(): pl.pallas_call(functools.partial(step_kernel, peers, slabs), out_shape=(p...  171 us
    pallas_call x1, Pallas kernels, write(): pl.pallas_call(write_kernel, out_shape=jax.ShapeDtypeStruct(fresh.shape,...  6.59 us

profile of v2, /device:TPU:0, one launch (start us, length us, event | category | flops | bytes accessed | tf_op | source)
XLA Modules:
  0.0 184.1 jit_solution(14039670051613462049)
XLA Ops:
  0.6 0.7 fusion.7
  1.3 0.2 convert_reduce_fusion
  1.5 0.0 copy-start.2
  1.5 0.7 select_reduce_fusion.holder_ref
  2.2 0.8 fusion.8
  3.1 0.1 copy.28
  3.2 0.0 copy-start
  3.2 0.6 slice_reduce_fusion
  3.8 0.7 stack.19
  4.5 0.9 fusion
  5.4 0.0 copy-done.2
  5.4 0.0 copy-done
  5.4 171.4 %shard_map.77 = (f32[2048,2048]{1,0:T(8,128)S(1)}, f32[256,128]{1,0:T(8,128)S(1)}, f32[192,8]{1,0:T(8,128)}) custom-call(s32[384]{0:T(512)} %select_reduce_fusion.holder_ref, s32[192]{0:T(256)} %copy-done.2, s32[192,8]{1,0:T(8,128)} %bitcast.17, bf16[192,8,1024]{2,1,0:T(8,128)(2,1)} %from_ref.1, s32[8,16,128]{2,1,0:T(8,128)} %bitcast.19, ...), custom_call_target="tpu_custom_call" | custom-call | flops 99999997952 | bytes 67108864 | tf_op jit(solution)/shard_map/pallas_call | solution.py:491
  176.8 0.0 copy-start.1
  176.8 6.6 %shard_map.78 = f32[2048,2048]{1,0:T(8,128)} custom-call(f32[256,128]{1,0:T(8,128)S(1)} %get-tuple-element.5.scale_ref, f32[2048,2048]{1,0:T(8,128)S(1)} %get-tuple-element.6.fresh_ref), custom_call_target="tpu_custom_call" | custom-call | tf_op jit(solution)/shard_map/pallas_call | solution.py:603
  183.4 0.0 copy-done.1
  183.4 0.7 copy.29
  (6 shorter events, 0.0 us)
Async XLA Ops:
  1.5 3.9 %copy-start.2 = (s32[192]{0:T(256)}, s32[192]{0:T(256)S(1)}, u32[]{:S(2)}) copy-start(s32[192]{0:T(256)S(1)} %fusion.6.slot_ref) | copy-start | bytes 2308
  3.2 2.3 %copy-start = (s32[192,8,1]{1,0,2:T(8,128)}, s32[192,8,1]{1,0,2:T(8,128)S(1)}, u32[]{:S(2)}) copy-start(s32[192,8,1]{1,0,2:T(8,128)S(1)} %copy.28) | copy-start | bytes 18436
  176.8 6.6 %copy-start.1 = (f32[192,8]{1,0:T(8,128)S(1)}, f32[192,8]{1,0:T(8,128)}, u32[]{:S(2)}) copy-start(f32[192,8]{1,0:T(8,128)} %get-tuple-element.15) | copy-start | bytes 18436
